TPU v7x, 32 devices: a 4x4x1 block of a 4x4x8 slice. The times are simulated.
32 devices in a mesh: rep: 2 (over z, core), dp: 16 (over x, y).
Axes of the slice: x: 4, y: 4, z: 1, core: 2. Of those that a mesh axis runs over, the one named last changes fastest.
The devices are a block of a 4x4x8 slice.
Arguments:
- x: bfloat16 [32, 2048, 640], P(('rep', 'dp')), parts along dimension 0
- dy: bfloat16 [32, 2048, 640], P(('rep', 'dp')), parts along dimension 0
- w_gate: bfloat16 [2, 640, 2048], replicated
- w_up: bfloat16 [2, 640, 2048], replicated
- w_down: bfloat16 [2, 2048, 640], replicated
- m_w_gate: float32 [2, 640, 2048], P(None, 'dp')
- m_w_up: float32 [2, 640, 2048], P(None, 'dp')
- m_w_down: float32 [2, 2048, 640], P(None, 'dp')
- v_w_gate: float32 [2, 640, 2048], P(None, 'dp')
- v_w_up: float32 [2, 640, 2048], P(None, 'dp')
- v_w_down: float32 [2, 2048, 640], P(None, 'dp')
Outputs:
- output 1: bfloat16 [4, 640, 2048], P('rep'), parts along dimension 0
- output 2: bfloat16 [4, 640, 2048], P('rep'), parts along dimension 0
- output 3: bfloat16 [4, 2048, 640], P('rep'), parts along dimension 0
- output 4: float32 [4, 640, 2048], P('rep', 'dp'), parts along dimension 0
- output 5: float32 [4, 640, 2048], P('rep', 'dp'), parts along dimension 0
- output 6: float32 [4, 2048, 640], P('rep', 'dp'), parts along dimension 0
- output 7: float32 [4, 640, 2048], P('rep', 'dp'), parts along dimension 0
- output 8: float32 [4, 640, 2048], P('rep', 'dp'), parts along dimension 0
- output 9: float32 [4, 2048, 640], P('rep', 'dp'), parts along dimension 0
There are 2 independent parts. A program takes and returns all parts, laid end to end along the dimension named above; an argument that names none is the same for every part.
All inputs are finite; a program needn't handle non-finite values.
Results may differ from a plain program's by a relative error of at most 0.022.
Values are sent between devices in bfloat16 or wider.
A program may use at most 768 MiB of HBM per device.

v0:
```python
import jax
import jax.numpy as jnp
from jax import lax

NAMES = ("w_gate", "w_up", "w_down")


def matmul(a, w):
    return jnp.dot(a, w, preferred_element_type=jnp.float32).astype(jnp.bfloat16)


def normed(h):
    wide = h.astype(jnp.float32)
    scale = lax.rsqrt(jnp.mean(wide**2, -1, keepdims=True) + 1e-6)
    return (wide * scale).astype(jnp.bfloat16)


def layer(h, w):
    a = normed(h)
    gate = jnp.dot(a, w["w_gate"], preferred_element_type=jnp.float32)
    up = jnp.dot(a, w["w_up"], preferred_element_type=jnp.float32)
    return h + matmul((jax.nn.silu(gate) * up).astype(jnp.bfloat16), w["w_down"])


def adamw(w, m, v, g):
    m = 0.9 * m + 0.1 * g
    v = 0.95 * v + 0.05 * g * g
    step = m * lax.rsqrt(v + 1e-8) + 0.1 * w
    return (w - 0.02 * step).astype(jnp.bfloat16), m, v


def clipped(gradients, sum_of_squares, count):
    factor = jnp.minimum(1.0, 0.5 * lax.rsqrt(sum_of_squares / count + 1e-30))
    return [g * factor for g in gradients]


def stack(weights, h):
    for number in range(weights["w_gate"].shape[0]):
        h = layer(h, {name: w[number] for name, w in weights.items()})
    return h


def solution(mesh):
    groups = mesh.shape["rep"]

    def step(x, dy, *arrays):
        weights, m, v = (arrays[i : i + 3] for i in (0, 3, 6))
        x, dy = (t.reshape(groups, -1, *t.shape[1:]) for t in (x, dy))

        def of_a_group(x, dy):
            _, back = jax.vjp(lambda w: stack(w, x), dict(zip(NAMES, weights, strict=True)))
            by_weights = back(dy)[0]
            gradients = [by_weights[name].astype(jnp.float32) for name in NAMES]
            gradients = clipped(gradients, sum(jnp.sum(g * g) for g in gradients), sum(g.size for g in gradients))
            new = [adamw(w.astype(jnp.float32), m, v, g) for w, m, v, g in zip(weights, m, v, gradients, strict=True)]
            return tuple(one[which] for which in range(3) for one in new)

        return tuple(t.reshape(-1, *t.shape[2:]) for t in jax.vmap(of_a_group)(x, dy))

    return step
```

profile of v0, /device:TPU:96, one launch (start us, length us, event | category | flops | bytes accessed | tf_op | source)
XLA Modules:
  0.0 775.6 jit_solution(11395846807774501516)
XLA Ops:
  7.2 0.1 reduce-scatter.27.cloned.1.call-start
  7.3 2.5 fusion.35
  9.7 4.4 copy
  14.2 8.5 %fusion.76 = f32[2048,2048]{1,0:T(8,128)S(1)} fusion(bf16[2,640,2048]{2,1,0:T(8,128)(2,1)} %param, bf16[1,2048,640]{2,1,0:T(8,128)(2,1)S(1)} %copy-done.1, f32[2048]{0:T(1024)S(1)} %add_rsqrt_fusion), kind=kOutput, calls=%fused_computation.88 | convolution fusion | flops 5372641280 | bytes 22028288 | tf_op jit(solution)/vmap(jvp())/dot_general | solution.py:20
  22.7 13.6 %fusion.74 = f32[2048,2048]{1,0:T(8,128)} fusion(bf16[2,640,2048]{2,1,0:T(8,128)(2,1)} %param.3, bf16[1,2048,640]{2,1,0:T(8,128)(2,1)S(1)} %copy-done.1, f32[2048]{0:T(1024)S(1)} %add_rsqrt_fusion), kind=kOutput, calls=%fused_computation.86 | convolution fusion | flops 5372641280 | bytes 22028288 | tf_op jit(solution)/vmap(jvp())/dot_general | solution.py:21
  36.3 8.6 %fusion.26 = bf16[2048,2048]{1,0:T(8,128)(2,1)S(1)} fusion(f32[2048,2048]{1,0:T(8,128)} %fusion.74, f32[2048,2048]{1,0:T(8,128)S(1)} %fusion.76), kind=kLoop, calls=%fused_computation.39 | loop fusion | flops 25165824 | bytes 41943040
  45.0 10.1 %fusion.39 = (f32[2048]{0:T(1024)S(1)}, bf16[1,1,2048,640]{2,3,1,0:T(8,128)(2,1)S(1)}) fusion(bf16[2048,2048]{1,0:T(8,128)(2,1)S(1)} %fusion.26, bf16[2,2048,640]{2,1,0:T(8,128)(2,1)} %param.4, bf16[1,2048,640]{1,2,0:T(8,128)(2,1)S(1)} %copy-done.11), kind=kOutput, calls=%fused_computation.56 | convolution fusion | flops 5375260672 | bytes 16261120 | tf_op jit(solution)/vmap(jvp())/dot_general | solution.py:9
  55.1 12.9 %fusion.63 = f32[2048,2048]{1,0:T(8,128)} fusion(bf16[2,640,2048]{2,1,0:T(8,128)(2,1)} %param, bf16[1,1,2048,640]{2,3,1,0:T(8,128)(2,1)S(1)} %get-tuple-element.10, f32[2048]{0:T(1024)S(1)} %bitcast.356), kind=kOutput, calls=%fused_computation.75 | convolution fusion | flops 5372641280 | bytes 22028288 | tf_op jit(solution)/vmap(jvp())/dot_general | solution.py:20
  68.0 12.1 %fusion.66 = f32[2048,2048]{1,0:T(8,128)} fusion(bf16[2,640,2048]{2,1,0:T(8,128)(2,1)} %param.3, bf16[1,1,2048,640]{2,3,1,0:T(8,128)(2,1)S(1)} %get-tuple-element.10, f32[2048]{0:T(1024)S(1)} %bitcast.357), kind=kOutput, calls=%fused_computation.78 | convolution fusion | flops 5372641280 | bytes 22028288 | tf_op jit(solution)/vmap(jvp())/dot_general | solution.py:21
  80.1 16.1 %fusion.42 = f32[1,2048,640]{2,1,0:T(8,128)} fusion(f32[2048,2048]{1,0:T(8,128)} %fusion.66, f32[2048,2048]{1,0:T(8,128)} %fusion.63, bf16[1,2048,640]{2,1,0:T(8,128)(2,1)S(1)} %copy-done.10), kind=kOutput, calls=%fused_computation.61 | convolution fusion | flops 5393874944 | bytes 41418752 | tf_op jit(solution)/vmap(transpose(jvp()))/dot_general | solution.py:9
  96.2 0.1 reduce-scatter.27.cloned.1.call-update
  96.3 0.1 reduce-scatter.29.cloned.1.call-start
  96.3 9.4 %convolution_convert_fusion.1 = bf16[2048,2048]{1,0:T(8,128)(2,1)S(1)} fusion(bf16[1,2048,640]{2,1,0:T(8,128)(2,1)S(1)} %copy-done.10, bf16[2,2048,640]{2,1,0:T(8,128)(2,1)} %param.4), kind=kOutput, calls=%fused_computation.48 | convolution fusion | flops 5372903424 | bytes 13631488 | tf_op jit(solution)/vmap(transpose(jvp()))/dot_general | solution.py:9
  105.7 3.2 copy-done.4
  108.9 15.8 %fusion.6 = bf16[2048,2048]{1,0:T(8,128)(2,1)} fusion(f32[2048,2048]{1,0:T(8,128)} %fusion.63, f32[2048,2048]{1,0:T(8,128)} %fusion.66, bf16[2048,2048]{1,0:T(8,128)(2,1)S(1)} %convolution_convert_fusion.1), kind=kLoop, calls=%fused_computation.11 | loop fusion | flops 50331648 | bytes 50331648
  124.8 3.0 copy.1
  127.8 13.2 %fusion.54 = bf16[2048,640]{0,1:T(8,128)(2,1)} fusion(bf16[2048,2048]{1,0:T(8,128)(2,1)} %copy-done.4, f32[2048,2048]{1,0:T(8,128)} %fusion.63, bf16[2,640,2048]{2,1,0:T(8,128)(2,1)} %param.3), kind=kOutput, calls=%fused_computation.66 | convolution fusion | flops 5395185664 | bytes 30408704 | tf_op jit(solution)/vmap(transpose(jvp()))/dot_general | solution.py:21
  141.0 8.2 %fusion.41 = (f32[2048]{0:T(1024)S(1)}, bf16[2048,640]{0,1:T(8,128)(2,1)S(1)}) fusion(bf16[1,1,2048,640]{2,3,1,0:T(8,128)(2,1)S(1)} %copy-done.7, bf16[2048,640]{0,1:T(8,128)(2,1)} %fusion.54, bf16[2048,2048]{1,0:T(8,128)(2,1)S(1)} %copy-done.3, bf16[2,640,2048]{2,1,0:T(8,128)(2,1)} %param), kind=kOutput, calls=%fused_computation.58 | convolution fusion | flops 5375260672 | bytes 18882560 | tf_op jit(solution)/vmap(transpose(jvp()))/dot_general | solution.py:20
  149.3 1.8 fusion.61
  151.1 1.5 copy-done.9
  152.6 11.0 %convolution_bitcast_fusion.1 = f32[1,2048,640]{2,1,0:T(8,128)} fusion(bf16[2048,2048]{1,0:T(8,128)(2,1)} %copy-done.2, bf16[2048,640]{0,1:T(8,128)(2,1)S(1)} %fusion.61), kind=kOutput, calls=%fused_computation.65 | convolution fusion | flops 5368709120 | bytes 16252928 | tf_op jit(solution)/vmap(transpose(jvp()))/dot_general | solution.py:9
  163.6 0.1 reduce-scatter.35.cloned.1.call-start
  163.7 1.6 copy-done.8
  165.3 13.0 %fusion.45 = f32[1,640,2048]{2,1,0:T(8,128)} fusion(bf16[2048,2048]{1,0:T(8,128)(2,1)} %copy-done.4, f32[2048,2048]{1,0:T(8,128)} %fusion.63, bf16[1,1,2048,640]{2,3,1,0:T(8,128)(2,1)S(1)} %copy-done.8, f32[2048]{0:T(1024)S(1)} %bitcast.359), kind=kOutput, calls=%fused_computation.62 | convolution fusion | flops 5397807104 | bytes 33038336 | tf_op jit(solution)/vmap(transpose(jvp()))/dot_general | solution.py:21
  178.4 0.1 reduce-scatter.37.cloned.1.call-start
  178.5 9.5 %convolution_convert_fusion = bf16[2048,2048]{1,0:T(8,128)(2,1)S(1)} fusion(bf16[2048,640]{0,1:T(8,128)(2,1)} %copy-done.9, bf16[2,2048,640]{2,1,0:T(8,128)(2,1)} %param.4), kind=kOutput, calls=%fused_computation.47 | convolution fusion | flops 5372903424 | bytes 13631488 | tf_op jit(solution)/vmap(transpose(jvp()))/dot_general | solution.py:9
  188.0 3.2 copy-done.20
  191.2 11.3 %fusion.51 = f32[1,640,2048]{2,1,0:T(8,128)} fusion(bf16[2048,2048]{1,0:T(8,128)(2,1)S(1)} %convolution_convert_fusion, f32[2048,2048]{1,0:T(8,128)} %copy-done, bf16[1,2048,640]{1,2,0:T(8,128)(2,1)S(1)} %copy-done.12, f32[2048]{0:T(1024)S(1)} %copy-done.18), kind=kOutput, calls=%fused_computation.64 | convolution fusion | flops 5397807104 | bytes 33038336 | tf_op jit(solution)/vmap(transpose(jvp()))/dot_general | solution.py:21
  202.6 0.1 reduce-scatter.31.cloned.1.call-start
  202.6 9.4 %convolution_bitcast_fusion = f32[1,640,2048]{2,1,0:T(8,128)} fusion(bf16[2048,2048]{1,0:T(8,128)(2,1)} %fusion.6, bf16[1,1,2048,640]{2,3,1,0:T(8,128)(2,1)S(1)} %copy-done.8, f32[2048]{0:T(1024)S(1)} %bitcast.360), kind=kOutput, calls=%fused_computation.60 | convolution fusion | flops 5372641280 | bytes 16261120 | tf_op jit(solution)/vmap(transpose(jvp()))/dot_general | solution.py:20
  212.2 0.1 reduce-scatter.33.cloned.1.call-start
  212.2 1.6 copy-done.13
  213.8 20.2 %fusion.48 = f32[1,640,2048]{2,1,0:T(8,128)} fusion(f32[2048,2048]{1,0:T(8,128)} %copy-done, f32[2048,2048]{1,0:T(8,128)} %fusion.74, bf16[2048,2048]{1,0:T(8,128)(2,1)} %copy-done.20, bf16[1,2048,640]{1,2,0:T(8,128)(2,1)S(1)} %copy-done.13, f32[2048]{0:T(1024)S(1)} %copy-done.18), kind=kOutput, calls=%fused_computation.63 | convolution fusion | flops 5418778624 | bytes 49815552 | tf_op jit(solution)/vmap(transpose(jvp()))/dot_general | solution.py:20
  234.0 0.1 reduce-scatter.33.cloned.1.call-update
  234.1 0.1 all-gather.14.cloned.1.call-start
  234.1 0.5 copy-done.19
  234.6 0.6 dynamic-slice
  235.9 1.0 convert_bitcast_fusion.4
  236.9 13.4 %reduce-scatter.29.cloned.1.call-done = f32[1,128,640]{2,1,0:T(8,128)} async-done(((f32[1,2048,640]{2,1,0:T(8,128)}), f32[1,128,640]{2,1,0:T(8,128)}) %reduce-scatter.29.cloned.1.call-update) | async-done | bytes 327696
  250.3 1.0 convert_bitcast_fusion.3
  251.3 0.8 fusion.113
  252.1 75.1 %reduce-scatter.35.cloned.1.call-done = f32[1,40,2048]{2,1,0:T(8,128)} async-done(((f32[1,640,2048]{2,1,0:T(8,128)}), f32[1,40,2048]{2,1,0:T(8,128)}) %reduce-scatter.35.cloned.1.call-update) | async-done | bytes 327696
  327.1 1.0 convert_bitcast_fusion.6
  328.1 76.2 %reduce-scatter.37.cloned.1.call-done = f32[1,40,2048]{2,1,0:T(8,128)} async-done(((f32[1,640,2048]{2,1,0:T(8,128)}), f32[1,40,2048]{2,1,0:T(8,128)}) %reduce-scatter.37.cloned.1.call-update) | async-done | bytes 327696
  404.3 1.0 convert_bitcast_fusion.5
  405.3 0.8 fusion.112
  406.1 75.4 %reduce-scatter.31.cloned.1.call-done = f32[1,40,2048]{2,1,0:T(8,128)} async-done(((f32[1,640,2048]{2,1,0:T(8,128)}), f32[1,40,2048]{2,1,0:T(8,128)}) %reduce-scatter.31.cloned.1.call-update) | async-done | bytes 327696
  481.5 1.0 convert_bitcast_fusion.8
  482.5 76.2 %reduce-scatter.33.cloned.1.call-done = f32[1,40,2048]{2,1,0:T(8,128)} async-done(((f32[1,640,2048]{2,1,0:T(8,128)}), f32[1,40,2048]{2,1,0:T(8,128)}) %reduce-scatter.33.cloned.1.call-update) | async-done | bytes 327696
  558.8 1.0 convert_bitcast_fusion.7
  559.8 0.8 fusion.111
  562.5 39.3 %all-reduce.16 = f32[1]{0:T(128)} all-reduce(f32[1]{0:T(128)} %bitcast.50), channel_id=5, replica_groups=mesh['rep'=2,'dp'=16] {'dp'}, use_global_device_ids=true, to_apply=%region_3.4.clone | all-reduce | flops 1 | bytes 8 | tf_op jit(solution)/vmap()/reduce_sum | solution.py:54
  602.5 2.5 fusion.130
  605.0 0.1 all-gather.14.cloned.1.call-update
  605.1 0.1 all-gather.10.cloned.1.call-start
  605.2 2.7 fusion.132
  607.9 0.1 all-gather.12.cloned.1.call-start
  608.0 2.9 fusion.131
  611.0 40.9 %all-gather.14.cloned.1.call-done = bf16[1,2,2048,640]{3,2,1,0:T(8,128)(2,1)} async-done(((bf16[1,2,128,640]{3,2,1,0:T(8,128)(2,1)}), bf16[1,2,2048,640]{3,2,1,0:T(8,128)(2,1)}) %all-gather.14.cloned.1.call-update) | async-done | bytes 5242896 | tf_op jit(solution)/reshape | solution.py:58
  651.8 53.0 %all-gather.10.cloned.1.call-done = bf16[1,2,640,2048]{3,2,1,0:T(8,128)(2,1)} async-done(((bf16[1,2,40,2048]{3,2,1,0:T(8,128)(2,1)}), bf16[1,2,640,2048]{3,2,1,0:T(8,128)(2,1)}) %all-gather.10.cloned.1.call-update) | async-done | bytes 5242896 | tf_op jit(solution)/reshape | solution.py:58
  704.8 53.0 %all-gather.12.cloned.1.call-done = bf16[1,2,640,2048]{3,2,1,0:T(8,128)(2,1)} async-done(((bf16[1,2,40,2048]{3,2,1,0:T(8,128)(2,1)}), bf16[1,2,640,2048]{3,2,1,0:T(8,128)(2,1)}) %all-gather.12.cloned.1.call-update) | async-done | bytes 5242896 | tf_op jit(solution)/reshape | solution.py:58
  757.8 6.2 copy.13
  763.9 2.4 copy.14
  766.3 2.4 copy.15
  (52 shorter events, 0.5 us)
Async XLA Ops:
  7.2 6.9 copy-start.1
  7.2 228.7 %reduce-scatter.27.cloned.1.call-start = ((), (), s32[]{:S(2)}) async-start(), calls=%async_computation.9 | async-start | bytes 5570560
  14.1 8.6 %copy-start.17 = (f32[2048]{0:T(1024)}, f32[2048]{0:T(1024)S(1)}, u32[]{:S(2)}) copy-start(f32[2048]{0:T(1024)S(1)} %add_rsqrt_fusion) | copy-start | bytes 24580
  22.7 13.6 %copy-start = (f32[2048,2048]{1,0:T(8,128)}, f32[2048,2048]{1,0:T(8,128)S(1)}, u32[]{:S(2)}) copy-start(f32[2048,2048]{1,0:T(8,128)S(1)} %fusion.76) | copy-start | bytes 50331652
  36.3 8.6 %copy-start.11 = (bf16[1,2048,640]{1,2,0:T(8,128)(2,1)S(1)}, bf16[1,2048,640]{1,2,0:T(8,128)(2,1)}, u32[]{:S(2)}) copy-start(bf16[1,2048,640]{1,2,0:T(8,128)(2,1)} %copy) | copy-start | bytes 7864324
  45.0 10.1 %copy-start.2 = (bf16[2048,2048]{1,0:T(8,128)(2,1)}, bf16[2048,2048]{1,0:T(8,128)(2,1)S(1)}, u32[]{:S(2)}) copy-start(bf16[2048,2048]{1,0:T(8,128)(2,1)S(1)} %fusion.26) | copy-start | bytes 25165828
  55.1 12.9 %copy-start.6 = (bf16[1,1,2048,640]{2,3,1,0:T(8,128)(2,1)}, bf16[1,1,2048,640]{2,3,1,0:T(8,128)(2,1)S(1)}, u32[]{:S(2)}) copy-start(bf16[1,1,2048,640]{2,3,1,0:T(8,128)(2,1)S(1)} %get-tuple-element.10) | copy-start | bytes 7864324
  68.0 12.1 %copy-start.10 = (bf16[1,2048,640]{2,1,0:T(8,128)(2,1)S(1)}, bf16[1,2048,640]{2,1,0:T(8,128)(2,1)}, u32[]{:S(2)}) copy-start(bf16[1,2048,640]{2,1,0:T(8,128)(2,1)} %param.5) | copy-start | bytes 7864324
  96.3 154.0 %reduce-scatter.29.cloned.1.call-start = ((), (), s32[]{:S(2)}) async-start(), calls=%async_computation.10 | async-start | bytes 5570560
  105.7 3.2 copy-start.4
  127.8 13.3 %copy-start.3 = (bf16[2048,2048]{1,0:T(8,128)(2,1)S(1)}, bf16[2048,2048]{1,0:T(8,128)(2,1)}, u32[]{:S(2)}) copy-start(bf16[2048,2048]{1,0:T(8,128)(2,1)} %fusion.6) | copy-start | bytes 25165828
  127.8 13.2 %copy-start.7 = (bf16[1,1,2048,640]{2,3,1,0:T(8,128)(2,1)S(1)}, bf16[1,1,2048,640]{2,3,1,0:T(8,128)(2,1)}, u32[]{:S(2)}) copy-start(bf16[1,1,2048,640]{2,3,1,0:T(8,128)(2,1)} %copy-done.6) | copy-start | bytes 7864324
  151.1 1.5 copy-start.9
  163.6 1.7 copy-start.8
  163.6 163.5 %reduce-scatter.35.cloned.1.call-start = ((), (), s32[]{:S(2)}) async-start(), calls=%async_computation.13 | async-start | bytes 5570560
  178.4 12.8 %copy-start.18 = (f32[2048]{0:T(1024)S(1)}, f32[2048]{0:T(1024)}, u32[]{:S(2)}) copy-start(f32[2048]{0:T(1024)} %copy-done.17) | copy-start | bytes 24580
  178.4 226.0 %reduce-scatter.37.cloned.1.call-start = ((), (), s32[]{:S(2)}) async-start(), calls=%async_computation.14 | async-start | bytes 5570560
  178.5 12.8 %copy-start.12 = (bf16[1,2048,640]{1,2,0:T(8,128)(2,1)S(1)}, bf16[1,2048,640]{1,2,0:T(8,128)(2,1)}, u32[]{:S(2)}) copy-start(bf16[1,2048,640]{1,2,0:T(8,128)(2,1)} %copy) | copy-start | bytes 7864324
  188.0 3.2 copy-start.20
  202.6 279.0 %reduce-scatter.31.cloned.1.call-start = ((), (), s32[]{:S(2)}) async-start(), calls=%async_computation.11 | async-start | bytes 5570560
  212.1 1.7 copy-start.13
  212.2 346.6 %reduce-scatter.33.cloned.1.call-start = ((), (), s32[]{:S(2)}) async-start(), calls=%async_computation.12 | async-start | bytes 5570560
  234.0 0.7 copy-start.19
  234.0 368.5 %copy-start.14 = (f32[2,128,640]{2,1,0:T(8,128)S(1)}, f32[2,128,640]{2,1,0:T(8,128)}, u32[]{:S(2)}) copy-start(f32[2,128,640]{2,1,0:T(8,128)} %param.10) | copy-start | bytes 1966084
  234.0 368.5 %copy-start.15 = (f32[2,128,640]{2,1,0:T(8,128)S(1)}, f32[2,128,640]{2,1,0:T(8,128)}, u32[]{:S(2)}) copy-start(f32[2,128,640]{2,1,0:T(8,128)} %param.9) | copy-start | bytes 1966084
  234.1 371.1 %copy-start.16 = (f32[2,40,2048]{2,1,0:T(8,128)S(1)}, f32[2,40,2048]{2,1,0:T(8,128)}, u32[]{:S(2)}) copy-start(f32[2,40,2048]{2,1,0:T(8,128)} %param.6) | copy-start | bytes 1966084
  234.1 417.8 %all-gather.14.cloned.1.call-start = ((), (), s32[]{:S(2)}) async-start(), calls=%async_computation.8 | async-start | bytes 5570560 | tf_op jit(solution)/reshape | solution.py:58
  605.1 99.7 %all-gather.10.cloned.1.call-start = ((), (), s32[]{:S(2)}) async-start(), calls=%async_computation.6 | async-start | bytes 5570560 | tf_op jit(solution)/reshape | solution.py:58
  607.9 149.8 %all-gather.12.cloned.1.call-start = ((), (), s32[]{:S(2)}) async-start(), calls=%async_computation.7 | async-start | bytes 5570560 | tf_op jit(solution)/reshape | solution.py:58
  757.8 6.2 copy-start.5
  757.8 8.5 %slice-start = ((s8[5242880]{0:T(1024)(128)(4,1)}), s8[4194304]{0:T(1024)(128)(4,1)S(1)}, s32[]{:S(2)}) async-start(s8[5242880]{0:T(1024)(128)(4,1)} %bitcast.348), calls=%async_computation.15 | async-start | bytes 8388608
  763.9 2.4 slice-start.1
Sparse Core Ops, SparseCore 0:
  96.4 76.9 reduce-scatter.26
  176.6 73.6 reduce-scatter.28
  253.5 73.5 reduce-scatter.34
  330.7 73.5 reduce-scatter.36
  408.0 73.5 reduce-scatter.30
  485.2 73.5 reduce-scatter.32
  605.2 46.6 all-gather.13
  654.4 50.3 all-gather.9
  707.3 50.3 all-gather.11
where the time goes:
time: 786 us; the launch traced here: 776 us
  waiting for transfers between devices  464 us (59%)
  matrix products  178 us (23%)
  other arithmetic  45.1 us (6%)
  blocking collectives  39.3 us (5%)
  local copies, waits for them, and re-layouts  30.6 us (4%)
  between operations  17.9 us (2%)
    unnamed x15, waiting for transfers between devices  317 us
    reshape x3, waiting for transfers between devices, step(): t.reshape(-1, *t.shape[2:])  147 us
    dot_general x5, matrix products, layer(): up = jnp.dot(a, w['w_up'], preferred_element_type=jnp.float32)  63.2 us
    dot_general x5, matrix products, layer(): gate = jnp.dot(a, w['w_gate'], preferred_element_type=jnp.float32)  59.3 us
    dot_general x5, matrix products, matmul(): jnp.dot(a, w, preferred_element_type=jnp.float32).astype(jnp.bfloat16)  56 us
    reduce_sum x1, blocking collectives, of_a_group(): jnp.sum(g * g)  39.3 us
    unnamed x51, local copies, waits for them, and re-layouts  30 us
    unnamed x4, other arithmetic  26.3 us
  transfers between devices with their start and end apart: 9, of which 8 were waited for; matrix products, arithmetic and copies ran while one was open for 18% of the time, Pallas kernels for 0%

commit v1 on v0

v1 whole, which is shorter than its diff:
```python
import functools
import math

import jax
import jax.numpy as jnp
from jax import lax
from jax.experimental import pallas as pl
from jax.experimental.pallas import tpu as pltpu
from jax.sharding import PartitionSpec as P

MESH = pl.DeviceIdType.MESH
F32, BF16 = jnp.float32, jnp.bfloat16
QUARTERS = 4
PIECES = 2
CHUNKS = 4
TILE = 512


NT = (((1,), (1,)), ((), ()))

def dot(a, b): return jnp.dot(a, b, preferred_element_type=F32)
def dot_nt(a, b): return lax.dot_general(a, b, NT, preferred_element_type=F32)

def normed(h):
    wide = h.astype(F32)
    scale = lax.rsqrt(jnp.mean(wide**2, -1, keepdims=True) + 1e-6)
    return (wide * scale).astype(BF16)

def forward_kernel(x, dy, wg, wu, wd, a0, a0t, h1, a1, a1t, dyt):
    a = normed(x[...])
    a0[...] = a
    a0t[...] = a.T
    dyt[...] = dy[...].T
    gate = dot(a, wg[...])
    up = dot(a, wu[...])
    p = (jax.nn.silu(gate) * up).astype(BF16)
    h = x[...] + dot(p, wd[...]).astype(BF16)
    h1[...] = h
    b = normed(h)
    a1[...] = b
    a1t[...] = b.T

def forward(x, dy, wg, wu, wd, T=256):
    n, d = x.shape
    f = wg.shape[2]
    tile = pl.BlockSpec((T, d), lambda i: (i, 0))
    tilet = pl.BlockSpec((d, T), lambda i: (0, i))
    const = lambda s: pl.BlockSpec((None, *s), lambda i: (0, 0, 0), pipeline_mode=pl.Buffered(1))
    S = jax.ShapeDtypeStruct
    return pl.pallas_call(
        forward_kernel, grid=(n // T,),
        in_specs=[tile, tile, const((d, f)), const((d, f)), const((f, d))],
        out_specs=[tile, tilet, tile, tile, tilet, tilet],
        out_shape=[S((n, d), BF16), S((d, n), BF16), S((n, d), BF16), S((n, d), BF16), S((d, n), BF16), S((d, n), BF16)],
        compiler_params=pltpu.CompilerParams(vmem_limit_bytes=60 * 2**20),
        name="fwd",
    )(x, dy, wg, wu, wd)


def tile_step(a, dy, wg, wu, wd):
    gate = dot(a, wg)
    up = dot(a, wu)
    dp = dot_nt(dy, wd).astype(BF16).astype(F32)
    s = jax.nn.sigmoid(gate)
    act = gate * s
    p = (act * up).astype(BF16)
    du = (dp * act).astype(BF16)
    dg = (dp * up * (s + act * (1.0 - s))).astype(BF16)
    return p, dg, du

def norm_back(h, da, dy):
    wide = h.astype(F32)
    d = h.shape[-1]
    scale = lax.rsqrt(jnp.mean(wide**2, -1, keepdims=True) + 1e-6)
    along = jnp.sum(da * wide, -1, keepdims=True)
    back = da * scale - wide * (along * (scale * scale * scale) * (1.0 / d))
    return (dy.astype(F32) + back.astype(BF16).astype(F32)).astype(BF16)

def adamw(w, m, v, g):
    m = 0.9 * m + 0.1 * g
    v = 0.95 * v + 0.05 * g * g
    step = m * lax.rsqrt(v + 1e-8) + 0.1 * w
    return (w - 0.02 * step).astype(BF16), m, v


class Torus:
    def __init__(self, side):
        self.side, self.n = side, side * side
        self.me = lax.axis_index("dp")
        self.row, self.col = lax.div(self.me, side), lax.rem(self.me, side)

    def greet(self):
        barrier = pltpu.get_barrier_semaphore()

        def one(k, _):
            pl.semaphore_signal(barrier, inc=1, device_id={"dp": lax.rem(self.me + k, self.n)}, device_id_type=MESH)
            return _

        lax.fori_loop(1, self.n, one, 0)
        pl.semaphore_wait(barrier, self.n - 1)

    def place(self, q):
        return (self.row, self.col) if q < 2 else (self.col, self.row)

    def wrap(self, k):
        return lax.rem(k + 2 * self.side, self.side)

    def device(self, q, u, v):
        u, v = self.wrap(u), self.wrap(v)
        return {"dp": u * self.side + v if q < 2 else v * self.side + u}

    def sign(self, q):
        return 1 if q % 2 == 0 else -1


def backward_kernel(side, layers, *refs):
    h1, a1, a1t, dy, dyt, a0, a0t, wg, wu, wd, sum_gu, sum_d, squares = refs[:13]
    (A, AT, DY, DYT, wgb, wub, wdb, ps, gs, us, das, loc_gu, loc_d, in1_gu, in1_d, in2_gu, in2_d, norms, tile) = refs[13:32]
    act_sem, w_sem, send_gu, recv_gu, send_d, recv_d, norm_send, norm_recv = refs[32:]
    here = Torus(side)
    place, wrap, device, sign = here.place, here.wrap, here.device, here.sign
    n, d = A.shape
    F = wgb.shape[2]
    T = TILE
    width = F // QUARTERS
    steps = side - 1
    last = layers - 1

    def weights(k):
        l, c, slot = last - lax.div(k, CHUNKS), lax.rem(k, CHUNKS), lax.rem(k, 2)
        cs = pl.ds(pl.multiple_of(c * F, F), F)
        return [
            pltpu.make_async_copy(wg.at[l, :, cs], wgb.at[slot], w_sem.at[slot, 0]),
            pltpu.make_async_copy(wu.at[l, :, cs], wub.at[slot], w_sem.at[slot, 1]),
            pltpu.make_async_copy(wd.at[l, cs], wdb.at[slot], w_sem.at[slot, 2]),
        ]

    loads = [pltpu.make_async_copy(x, y, act_sem.at[k]) for k, (x, y) in enumerate(((a1, A), (dy, DY), (a1t, AT), (dyt, DYT)))]
    for one in (loads[0], loads[1], *weights(0), loads[2], loads[3]):
        one.start()
    here.greet()
    tile[...] = jnp.zeros_like(tile)
    das[...] = jnp.zeros_like(das)
    for one in loads:
        one.wait()

    def strip(q):
        return pl.ds(q * (d // QUARTERS), d // QUARTERS)

    def lanes(k, q):
        return pl.ds(pl.multiple_of((lax.rem(k, CHUNKS) * QUARTERS + q) * width, 128), width)

    def sems(gu, k, q, s):
        return (send_gu.at[k, q, s], recv_gu.at[k, q, s]) if gu else (send_d.at[k, q, s], recv_d.at[k, q, s])

    def local_unit(gu, k, q, u):
        if not gu:
            return loc_d.at[k, u, :, strip(q)] if q < 2 else loc_d.at[k, :, u, strip(q)]
        return loc_gu.at[:, u, :, :, lanes(k, q)] if q < 2 else loc_gu.at[:, :, u, :, lanes(k, q)]

    def first(gu, k, q, s):
        mu, mv = place(q)
        g = sign(q)
        ins = in1_gu if gu else in1_d
        src = local_unit(gu, k, q, wrap(mu - g)) if s == 0 else ins.at[k, q, s - 1]
        a, b = sems(gu, k, q, s)
        return pltpu.make_async_remote_copy(src, ins.at[k, q, s], a, b, device_id=device(q, mu + g, mv), device_id_type=MESH)

    def second(gu, k, q, s):
        mu, mv = place(q)
        g = sign(q)
        ins = in2_gu if gu else in2_d
        if s == 0:
            v = wrap(mv - g)
            src = in1_gu.at[k, q, steps - 1, :, v] if gu else in1_d.at[k, q, steps - 1, v]
        else:
            src = ins.at[k, q, s - 1]
        a, b = sems(gu, k, q, steps + s)
        return pltpu.make_async_remote_copy(src, ins.at[k, q, s], a, b, device_id=device(q, mu, mv + g), device_id_type=MESH)

    def add_first(gu, k, q, s):
        u = wrap(place(q)[0] - sign(q) * (s + 2))

        def one(v, _):
            a, b = (u, v) if q < 2 else (v, u)
            if gu:
                mine = loc_gu[:, a, b, :, lanes(k, q)].astype(F32)
                in1_gu[k, q, s, :, v] = (in1_gu[k, q, s, :, v].astype(F32) + mine).astype(BF16)
            else:
                mine = loc_d[k, a, b, strip(q)].astype(F32)
                in1_d[k, q, s, v] = (in1_d[k, q, s, v].astype(F32) + mine).astype(BF16)
            return _

        lax.fori_loop(0, side, one, 0)

    def add_second(gu, k, q, s):
        v = wrap(place(q)[1] - sign(q) * (s + 2))
        if gu:
            total = (in2_gu[k, q, s].astype(F32) + in1_gu[k, q, steps - 1, :, v].astype(F32)).astype(BF16)
        else:
            total = (in2_d[k, q, s].astype(F32) + in1_d[k, q, steps - 1, v].astype(F32)).astype(BF16)
        if s < steps - 1:
            if gu:
                in2_gu[k, q, s] = total
            else:
                in2_d[k, q, s] = total
            return
        total = total.astype(F32)
        if gu:
            sum_gu[:, last - lax.div(k, CHUNKS), :, lanes(k, q)] = total
        else:
            sum_d[k, strip(q)] = total
        square = total * total
        square = square.reshape(-1, 8, square.shape[-1]).sum(0)
        tile[...] += sum(square[:, i : i + 128] for i in range(0, square.shape[-1], 128))

    def begin(gu, k):
        for q in range(QUARTERS):
            first(gu, k, q, 0).start()

    def advance(gu, k, s):
        for q in range(QUARTERS):
            if s < steps:
                first(gu, k, q, s).wait()
                add_first(gu, k, q, s)
                (first(gu, k, q, s + 1) if s + 1 < steps else second(gu, k, q, 0)).start()
            else:
                second(gu, k, q, s - steps).wait()
                add_second(gu, k, q, s - steps)
                if s + 1 < 2 * steps:
                    second(gu, k, q, s - steps + 1).start()

    def chunk(k, inner):
        slot, c = lax.rem(k, 2), lax.rem(k, CHUNKS)
        for one in weights(k):
            one.wait()

        @pl.when(k + 1 < layers * CHUNKS)
        def _():
            for one in weights(k + 1):
                one.start()

        def ticks(s):
            for back, more in ((1, 0), (2, steps)):
                if inner:
                    pl.when(k >= back)(lambda: advance(True, k - back, s + more))
                else:
                    advance(True, k - back, s + more)

        for t in range(n // T):
            ts = pl.ds(t * T, T)
            p, dg, du = tile_step(A[ts], DY[ts], wgb[slot], wub[slot], wdb[slot])
            ps[ts] = p
            gs[ts] = dg
            us[ts] = du
            if inner:
                das[ts] += dot_nt(dg, wgb[slot]) + dot_nt(du, wub[slot])
            if t % 2 == 1:
                ticks(t // 2)
        cs = pl.ds(pl.multiple_of(c * F, F), F)
        rows = loc_gu.shape[3]
        for which, of in ((0, gs), (1, us)):
            g = dot(AT[...], of[...]).astype(BF16)
            for i in range(side * side):
                loc_gu[which, i // side, i % side, :, cs] = g[i * rows : (i + 1) * rows]
        l = last - lax.div(k, CHUNKS)
        g = dot(DYT[...], ps[...]).astype(BF16)
        wide = loc_d.shape[4]
        for i in range(F // wide):
            to = c * (F // wide) + i
            loc_d[l, lax.div(to, side), lax.rem(to, side)] = g[:, i * wide : (i + 1) * wide]
        ticks(steps - 1)
        begin(True, k)

    lax.fori_loop(0, CHUNKS, lambda k, _: (chunk(k, True), _)[1], 0)
    begin(False, last)

    again = [pltpu.make_async_copy(x, y, act_sem.at[k]) for k, (x, y) in enumerate(((h1, A), (a0, A), (a0t, AT)))]
    again[0].start()
    again[2].start()
    again[0].wait()

    def turn(t, _):
        ts = pl.ds(pl.multiple_of(t * 256, 256), 256)
        r = norm_back(A[ts], das[ts].astype(BF16).astype(F32), DY[ts])
        DY[ts] = r
        DYT[:, ts] = r.T
        return _

    lax.fori_loop(0, n // 256, turn, 0)
    again[1].start()
    again[1].wait()
    again[2].wait()

    def outer(k, _):
        chunk(k, False)
        for i in range(CHUNKS):
            pl.when(k == CHUNKS + i)(lambda: advance(False, last, i))
        return _

    lax.fori_loop(CHUNKS, 2 * CHUNKS, outer, 0)
    begin(False, 0)
    end = 2 * CHUNKS - 1
    for s in range(2 * steps):
        if s < steps:
            advance(True, end - 1, steps + s)
        advance(True, end, s)
        if CHUNKS + s < 2 * steps:
            advance(False, last, CHUNKS + s)
        advance(False, 0, s)

    norms[here.me] = tile[...]

    def share(k):
        return pltpu.make_async_remote_copy(
            tile, norms.at[here.me], norm_send.at[k], norm_recv.at[k],
            device_id={"dp": lax.rem(here.me + k, here.n)}, device_id_type=MESH)

    lax.fori_loop(1, here.n, lambda k, _: (share(k).start(), _)[1], 0)
    lax.fori_loop(1, here.n, lambda k, _: (share(k).wait(), _)[1], 0)
    squares[...] = jnp.sum(norms[...], axis=0)


def backward(side, layers, acts, weights, rows, deep):
    n, d = acts[0].shape
    f = weights[0].shape[2]
    F = f // CHUNKS
    width = F // QUARTERS
    steps = side - 1
    S, V = jax.ShapeDtypeStruct, pltpu.VMEM
    jobs = layers * CHUNKS
    vmem, hbm = pl.BlockSpec(memory_space=pltpu.VMEM), pl.BlockSpec(memory_space=pl.ANY)
    return pl.pallas_call(
        functools.partial(backward_kernel, side, layers),
        out_shape=[S((2, layers, rows, f), F32), S((layers, d, deep), F32), S((8, 128), F32)],
        in_specs=[hbm] * 10,
        out_specs=[vmem] * 3,
        scratch_shapes=[
            V((n, d), BF16), V((d, n), BF16), V((n, d), BF16), V((d, n), BF16),
            V((2, d, F), BF16), V((2, d, F), BF16), V((2, F, d), BF16),
            V((n, F), BF16), V((n, F), BF16), V((n, F), BF16), V((n, d), F32),
            V((2, side, side, rows, f), BF16),
            V((layers, side, side, d, deep), BF16),
            V((jobs, QUARTERS, steps, 2, side, rows, width), BF16),
            V((layers, QUARTERS, steps, side, d // QUARTERS, deep), BF16),
            V((jobs, QUARTERS, steps, 2, rows, width), BF16),
            V((layers, QUARTERS, steps, d // QUARTERS, deep), BF16),
            V((side * side, 8, 128), F32), V((8, 128), F32),
            pltpu.SemaphoreType.DMA((4,)),
            pltpu.SemaphoreType.DMA((2, 3)),
            pltpu.SemaphoreType.DMA((jobs, QUARTERS, 2 * steps)),
            pltpu.SemaphoreType.DMA((jobs, QUARTERS, 2 * steps)),
            pltpu.SemaphoreType.DMA((layers, QUARTERS, 2 * steps)),
            pltpu.SemaphoreType.DMA((layers, QUARTERS, 2 * steps)),
            pltpu.SemaphoreType.DMA((side * side,)),
            pltpu.SemaphoreType.DMA((side * side,)),
        ],
        compiler_params=pltpu.CompilerParams(collective_id=0, has_side_effects=True, vmem_limit_bytes=67043328),
        name="bwd",
    )(*acts, *weights)


def gather_kernel(side, layers, count, *refs):
    sum_gu, sum_d, squares, w_gate, w_up, w_down, m_gate, m_up, m_down, v_gate, v_up, v_down = refs[:12]
    new_gu, new_d, nm_gate, nm_up, nm_down, nv_gate, nv_up, nv_down = refs[12:20]
    own_gu, own_d, old_gu, old_d, send_gu, recv_gu, send_d, recv_d, keep_sem = refs[20:]
    here = Torus(side)
    place, wrap, device, sign, me, row, col = here.place, here.wrap, here.device, here.sign, here.me, here.row, here.col
    steps = side - 1
    rows, cols = m_gate.shape[1:]
    deep = m_down.shape[1]
    width = cols // PIECES // QUARTERS
    at, deep_at = pl.ds(pl.multiple_of(me * rows, 8), rows), pl.ds(pl.multiple_of(me * deep, 8), deep)
    olds = [
        pltpu.make_async_copy(w_gate.at[:, at], old_gu.at[0], keep_sem.at[0, 0]),
        pltpu.make_async_copy(w_up.at[:, at], old_gu.at[1], keep_sem.at[0, 1]),
        pltpu.make_async_copy(w_down.at[:, deep_at], old_d, keep_sem.at[1, 0]),
    ]
    for one in olds:
        one.start()
    here.greet()
    for one in olds:
        one.wait()

    def lanes(h, q):
        return pl.ds(pl.multiple_of((h * QUARTERS + q) * width, 128), width)

    def sems(l, h, q, s):
        if h is None:
            return send_d.at[l, q, s], recv_d.at[l, q, s]
        return send_gu.at[l, h, q, s], recv_gu.at[l, h, q, s]

    def jobs(f):
        for l in reversed(range(layers)):
            lax.fori_loop(0, PIECES, lambda h, _: (f(l, h), _)[1], 0)
            f(l, None)

    total = jnp.sum(squares[...])
    factor = jnp.minimum(1.0, 0.5 * lax.rsqrt(jnp.full((1, 128), total, F32) / count + 1e-30))

    def gather(l, h, q, s):
        mu, mv = place(q)
        g = sign(q)
        if s < steps:
            v = wrap(mv - g * s)
            a, b = (mu, v) if q < 2 else (v, mu)
            dst = new_d.at[l, a, b, q] if h is None else new_gu.at[:, l, a, b, :, lanes(h, q)]
            src = dst
            if s == 0:
                src = own_d.at[l, q] if h is None else own_gu.at[:, l, :, lanes(h, q)]
            to = device(q, mu, mv + g)
        else:
            u = wrap(mu - g * (s - steps))
            if h is None:
                dst = new_d.at[l, u, :, q] if q < 2 else new_d.at[l, :, u, q]
            else:
                at = lanes(h, q)
                dst = new_gu.at[:, l, u, :, :, at] if q < 2 else new_gu.at[:, l, :, u, :, at]
            src = dst
            to = device(q, mu + g, mv)
        a, b = sems(l, h, q, s)
        return pltpu.make_async_remote_copy(src, dst, a, b, device_id=to, device_id_type=MESH)

    def keep(l, d):
        if d:
            return pltpu.make_async_copy(own_d.at[l], new_d.at[l, row, col], keep_sem.at[l, 1])
        return pltpu.make_async_copy(own_gu.at[:, l], new_gu.at[:, l, row, col], keep_sem.at[l, 0])

    for l in reversed(range(layers)):
        for h in range(PIECES):
            for q in range(QUARTERS):
                at = pl.ds((h * QUARTERS + q) * width, width)
                by = jnp.tile(factor, (1, width // 128))
                for k, (w, m, v, nm, nv) in enumerate(((old_gu.at[0], m_gate, v_gate, nm_gate, nv_gate), (old_gu.at[1], m_up, v_up, nm_up, nv_up))):
                    new, nm[l, :, at], nv[l, :, at] = adamw(
                        w[l, :, at].astype(F32), m[l, :, at], v[l, :, at], sum_gu[k, l, :, at] * by)
                    own_gu[k, l, :, at] = new
                gather(l, h, q, 0).start()
        keep(l, False).start()
        turned = sum_d[l].T
        for q in range(QUARTERS):
            rows = m_down.shape[1] // QUARTERS
            at = pl.ds(q * rows, rows)
            by = jnp.tile(factor, (1, m_down.shape[2] // 128))
            new, nm_down[l, at], nv_down[l, at] = adamw(
                old_d[l, at].astype(F32), m_down[l, at], v_down[l, at], turned[q * rows : (q + 1) * rows] * by)
            own_d[l, q] = new
            gather(l, None, q, 0).start()
        keep(l, True).start()
    for l in reversed(range(layers)):
        keep(l, False).wait()
        keep(l, True).wait()
    for s in range(2 * steps):
        def advance(l, h, s=s):
            for q in range(QUARTERS):
                gather(l, h, q, s).wait()
                if s + 1 < 2 * steps:
                    gather(l, h, q, s + 1).start()

        jobs(advance)


def gather(side, sums, w, m, v):
    layers, rows, cols = m[0].shape
    deep, narrow = m[2].shape[1:]
    quarter = deep // QUARTERS
    n = side * side
    steps = side - 1
    count = layers * n * (2 * rows * cols + deep * narrow)
    vmem, hbm = pl.BlockSpec(memory_space=pltpu.VMEM), pl.BlockSpec(memory_space=pl.ANY)
    outs = pl.pallas_call(
        functools.partial(gather_kernel, side, layers, count),
        out_shape=[
            jax.ShapeDtypeStruct((2, layers, side, side, rows, cols), BF16),
            jax.ShapeDtypeStruct((layers, side, side, QUARTERS, quarter, narrow), BF16),
            *(jax.ShapeDtypeStruct(t.shape, F32) for t in (*m, *v)),
        ],
        in_specs=[vmem] * 3 + [hbm] * 3 + [vmem] * 6,
        out_specs=[hbm] * 2 + [vmem] * 6,
        scratch_shapes=[
            pltpu.VMEM((2, layers, rows, cols), BF16),
            pltpu.VMEM((layers, QUARTERS, quarter, narrow), BF16),
            pltpu.VMEM((2, layers, rows, cols), BF16),
            pltpu.VMEM((layers, deep, narrow), BF16),
            pltpu.SemaphoreType.DMA((layers, PIECES, QUARTERS, 2 * steps)),
            pltpu.SemaphoreType.DMA((layers, PIECES, QUARTERS, 2 * steps)),
            pltpu.SemaphoreType.DMA((layers, QUARTERS, 2 * steps)),
            pltpu.SemaphoreType.DMA((layers, QUARTERS, 2 * steps)),
            pltpu.SemaphoreType.DMA((layers, 2)),
        ],
        compiler_params=pltpu.CompilerParams(collective_id=1, has_side_effects=True, vmem_limit_bytes=40 * 2**20),
        name="gather",
    )(*sums, *w, *m, *v)
    gu = outs[0].reshape(2, layers, n * rows, cols)
    return (gu[0], gu[1], outs[1].reshape(layers, n * deep, narrow), *outs[2:])


def solution(mesh):
    side = math.isqrt(mesh.shape["dp"])

    def step(x, dy, *arrays):
        weights, m, v = (arrays[i : i + 3] for i in (0, 3, 6))
        layers = weights[0].shape[0]

        a0, a0t, h1, a1, a1t, dyt = forward(x[0], dy[0], *weights)
        acts = (h1, a1, a1t, dy[0], dyt, a0, a0t)
        sums = backward(side, weights[0].shape[0], acts, weights, m[0].shape[1], m[2].shape[1])
        return gather(side, sums, weights, m, v)

    whole, block = P(None, None, None), P(None, "dp", None)
    return jax.shard_map(
        step,
        mesh=mesh,
        in_specs=(P(("rep", "dp"), None, None),) * 2 + (whole,) * 3 + (block,) * 6,
        out_specs=(P("rep", None, None),) * 3 + (P("rep", "dp", None),) * 6,
        check_vma=False,
    )
```

time: 786 us -> 311 us (0.40); the launches traced: 776 us -> 310 us
  waiting for transfers between devices: 464 us -> 0 us
  Pallas kernels: 0 us -> 278 us
  matrix products: 178 us -> 0 us
  other arithmetic: 45.1 us -> 0 us
  blocking collectives: 39.3 us -> 0 us
  between operations: 17.9 us -> 0.69 us
    unnamed x15 -> x0, waiting for transfers between devices: 317 us -> none
    pallas_call x0 -> x3, Pallas kernels: none -> 278 us  [the longest x1 172 us: backward(): pl.pallas_call(functools.partial(backward_kernel, side, layers), out_shap...]
    dot_general x15 -> x0, matrix products: 178 us -> none  [the longest x5 63.2 us: layer(): up = jnp.dot(a, w['w_up'], preferred_element_type=jnp.float32)]
    reshape x3 -> x0, waiting for transfers between devices: 147 us -> none  [step(): t.reshape(-1, *t.shape[2:])]
    reduce_sum x1 -> x0, blocking collectives: 39.3 us -> none  [of_a_group(): jnp.sum(g * g)]
    unnamed x4 -> x0, other arithmetic: 26.3 us -> none
    slice x0 -> x1, local copies, waits for them, and re-layouts: none -> 10.3 us  [gather(): return (gu[0], gu[1], outs[1].reshape(layers, n * deep, narrow), *outs[2:])]
    unnamed x51 -> x29, local copies, waits for them, and re-layouts: 30 us -> 20.8 us
  transfers between devices with their start and end apart: 9 -> 0, of which waited for: 8 -> 0; matrix products, arithmetic and copies ran while one was open for 18% -> 0% of each run, Pallas kernels for 0% -> 0%
where the time goes in v1:
time: 311 us; the launch traced here: 310 us
  Pallas kernels  278 us (89%)
  local copies, waits for them, and re-layouts  31.1 us (10%)
    pallas_call x1, Pallas kernels, backward(): pl.pallas_call(functools.partial(backward_kernel, side, layers), out_shap...  172 us
    pallas_call x1, Pallas kernels, gather(): pl.pallas_call(functools.partial(gather_kernel, side, layers, count), out...  78.3 us
    pallas_call x1, Pallas kernels, forward(): pl.pallas_call(forward_kernel, grid=(n // T,), in_specs=[tile, tile, cons...  27.9 us
    unnamed x29, local copies, waits for them, and re-layouts  20.8 us
    slice x1, local copies, waits for them, and re-layouts, gather(): return (gu[0], gu[1], outs[1].reshape(layers, n * deep, narrow), *outs[2:])  10.3 us

profile of v1, /device:TPU:96, one launch (start us, length us, event | category | flops | bytes accessed | tf_op | source)
XLA Modules:
  0.0 310.3 jit_solution(10345564530978208254)
XLA Ops:
  0.6 27.9 %fwd.1 = (bf16[2048,640]{1,0:T(8,128)(2,1)}, bf16[640,2048]{1,0:T(8,128)(2,1)}, bf16[2048,640]{1,0:T(8,128)(2,1)}, bf16[2048,640]{1,0:T(8,128)(2,1)}, bf16[640,2...) custom-call(bf16[2048,640]{1,0:T(8,128)(2,1)} %bitcast.10, bf16[2048,640]{1,0:T(8,128)(2,1)} %bitcast.5, ...), custom_call_target="tpu_custom_call" | custom-call | tf_op jit(solution)/shard_map/fwd/pallas_call | solution.py:50
  28.5 172.3 %bwd.1 = (f32[2,2,40,2048]{3,2,1,0:T(8,128)}, f32[2,640,128]{2,1,0:T(8,128)}, f32[8,128]{1,0:T(8,128)}) custom-call(bf16[2048,640]{1,0:T(8,128)(2,1)} %get-tuple-element.26.refs_0_, bf16[2048,640]{1,0:T(8,128)(2,1)} %get-tuple-element.27.refs_1_, bf16[640,2048]{1,0:T(8,128)(2,1)} %get-tuple-element.28.refs_2_, bf16[2048,640]{1,0:T(8,128)(2,1)} %bitcast.6, ...), custom_call_target="tpu_custom_call" | custom-call | tf_op jit(solution)/shard_map/bwd/pallas_call | solution.py:333
  200.8 0.0 copy-start
  200.9 1.3 copy-done
  202.2 0.0 copy-start.1
  202.2 1.1 copy-done.1
  203.2 0.0 copy-start.2
  203.3 1.1 copy-done.2
  204.3 0.0 copy-start.3
  204.3 1.1 copy-done.3
  205.4 0.0 copy-start.4
  205.4 1.1 copy-done.4
  206.5 0.0 copy-start.5
  206.5 1.1 copy-done.5
  207.6 0.0 copy-start.6
  207.6 1.1 copy-done.6
  208.7 0.0 copy-start.7
  208.7 1.1 copy-done.7
  209.8 0.0 copy-start.10
  209.8 0.7 copy-done.10
  210.5 78.3 %gather.1 = (bf16[2,2,4,4,40,2048]{5,4,3,2,1,0:T(8,128)(2,1)}, bf16[2,4,4,4,32,640]{5,4,3,2,1,0:T(8,128)(2,1)}, f32[2,40,2048]{2,1,0:T(8,128)S(1)}, f32[2,40,204...) custom-call(f32[2,2,40,2048]{3,2,1,0:T(8,128)S(1)} %copy-done, ...), custom_call_target="tpu_custom_call" | custom-call | tf_op jit(solution)/shard_map/gather/pallas_call | solution.py:471
  288.8 0.0 copy-start.8
  288.8 0.8 copy-done.8
  289.6 10.3 %fusion = (bf16[1,2,4,4,40,2048]{5,4,3,2,1,0:T(8,128)(2,1)}, bf16[1,2,4,4,40,2048]{5,4,3,2,1,0:T(8,128)(2,1)}) fusion(bf16[2,2,4,4,40,2048]{5,4,3,2,1,0:T(8,128)(2,1)} %get-tuple-element.35), kind=kLoop, calls=%fused_computation | loop fusion | bytes 20971520 | tf_op jit(solution)/shard_map/slice | solution.py:495
  299.9 0.0 copy-start.9
  299.9 5.4 %copy.27 = bf16[2,2048,640]{2,1,0:T(8,128)(2,1)} copy(bf16[2,2048,640]{2,1,0:T(8,128)(2,1)} %bitcast.9) | data formatting | bytes 10485760
  305.3 0.0 copy-done.9
  305.3 0.8 copy.28
  306.1 0.8 copy.29
  307.0 0.8 copy.30
  307.8 0.8 copy.31
  308.6 0.8 copy.32
  309.5 0.8 copy.33
Async XLA Ops:
  200.8 1.3 copy-start
  202.2 1.1 copy-start.1
  203.2 1.1 copy-start.2
  204.3 1.1 copy-start.3
  205.4 1.1 copy-start.4
  206.5 1.1 copy-start.5
  207.6 1.1 copy-start.6
  208.7 1.1 copy-start.7
  209.8 0.7 copy-start.10
  288.8 0.8 copy-start.8
  299.9 5.4 %copy-start.9 = (f32[2,40,2048]{2,1,0:T(8,128)S(1)}, f32[2,40,2048]{2,1,0:T(8,128)}, u32[]{:S(2)}) copy-start(f32[2,40,2048]{2,1,0:T(8,128)} %copy-done.8) | copy-start | bytes 1966084

commit v2 on v1

--- a/solution.py
+++ b/solution.py
@@ -14,6 +14,7 @@
 PIECES = 2
 CHUNKS = 4
 TILE = 512
+STEPS_AT = (((3, 3), (2, 1)), ((3, 4), (1, 0)), ((3, 5), (2, 2)))
 
 
 NT = (((1,), (1,)), ((), ()))
@@ -141,7 +142,7 @@
     here.greet()
     tile[...] = jnp.zeros_like(tile)
     das[...] = jnp.zeros_like(das)
-    for one in loads:
+    for one in loads[:2]:
         one.wait()
 
     def strip(q):
@@ -240,12 +241,12 @@
             for one in weights(k + 1):
                 one.start()
 
-        def ticks(s):
-            for back, more in ((1, 0), (2, steps)):
+        def ticks(point):
+            for back, step in STEPS_AT[point]:
                 if inner:
-                    pl.when(k >= back)(lambda: advance(True, k - back, s + more))
+                    pl.when(k >= back)(lambda: advance(True, k - back, step))
                 else:
-                    advance(True, k - back, s + more)
+                    advance(True, k - back, step)
 
         for t in range(n // T):
             ts = pl.ds(t * T, T)
@@ -257,6 +258,12 @@
                 das[ts] += dot_nt(dg, wgb[slot]) + dot_nt(du, wub[slot])
             if t % 2 == 1:
                 ticks(t // 2)
+        if inner:
+            @pl.when(k == 0)
+            def _():
+                for one in loads[2:]:
+                    one.wait()
+
         cs = pl.ds(pl.multiple_of(c * F, F), F)
         rows = loc_gu.shape[3]
         for which, of in ((0, gs), (1, us)):
@@ -269,7 +276,7 @@
         for i in range(F // wide):
             to = c * (F // wide) + i
             loc_d[l, lax.div(to, side), lax.rem(to, side)] = g[:, i * wide : (i + 1) * wide]
-        ticks(steps - 1)
+        ticks(2)
         begin(True, k)
 
     lax.fori_loop(0, CHUNKS, lambda k, _: (chunk(k, True), _)[1], 0)
@@ -302,12 +309,9 @@
     begin(False, 0)
     end = 2 * CHUNKS - 1
     for s in range(2 * steps):
-        if s < steps:
-            advance(True, end - 1, steps + s)
-        advance(True, end, s)
-        if CHUNKS + s < 2 * steps:
-            advance(False, last, CHUNKS + s)
-        advance(False, 0, s)
+        for gu, k, done in ((True, end - 2, 3), (False, last, CHUNKS), (True, end - 1, 1), (True, end, 0), (False, 0, 0)):
+            if done + s < 2 * steps:
+                advance(gu, k, done + s)
 
     norms[here.me] = tile[...]
 
@@ -360,27 +364,54 @@
     )(*acts, *weights)
 
 
-def gather_kernel(side, layers, count, *refs):
-    sum_gu, sum_d, squares, w_gate, w_up, w_down, m_gate, m_up, m_down, v_gate, v_up, v_down = refs[:12]
-    new_gu, new_d, nm_gate, nm_up, nm_down, nv_gate, nv_up, nv_down = refs[12:20]
-    own_gu, own_d, old_gu, old_d, send_gu, recv_gu, send_d, recv_d, keep_sem = refs[20:]
+def adam_kernel(count, me, gate, up, down, sum_gu, sum_d, squares, *refs):
+    m, v, own, nm, nv = refs[:3], refs[3:6], refs[6:8], refs[8:11], refs[11:]
+    total = jnp.sum(squares[...])
+    factor = jnp.minimum(1.0, 0.5 * lax.rsqrt(jnp.full((1, 1), total, F32) / count + 1e-30))
+    for k, w in enumerate((gate, up)):
+        own[0][k], nm[k][...], nv[k][...] = adamw(w[...].astype(F32), m[k][...], v[k][...], sum_gu[k] * factor)
+    own[1][...], nm[2][...], nv[2][...] = adamw(down[...].astype(F32), m[2][...], v[2][...], sum_d[...].T * factor)
+
+
+def adam(sums, w, m, v, n):
+    layers, rows, cols = m[0].shape
+    deep, narrow = m[2].shape[1:]
+    S = jax.ShapeDtypeStruct
+    wide, tall = (None, rows, cols), (None, deep, narrow)
+    mine = lambda s: pl.BlockSpec(s, lambda l, me: (l, me[0], 0))
+    whole = lambda s: pl.BlockSpec(s, lambda l, me: (l, 0, 0))
+    both = pl.BlockSpec((2, None, rows, cols), lambda l, me: (0, l, 0, 0))
+    moments = [whole(wide), whole(wide), whole(tall)]
+    outs = pl.pallas_call(
+        functools.partial(adam_kernel, layers * n * (2 * rows * cols + deep * narrow)),
+        grid_spec=pltpu.PrefetchScalarGridSpec(
+            num_scalar_prefetch=1,
+            grid=(layers,),
+            in_specs=[mine(wide), mine(wide), mine(tall), both, whole((None, narrow, deep)), pl.BlockSpec((8, 128), lambda l, me: (0, 0)), *moments, *moments],
+            out_specs=[both, whole(tall), *moments, *moments],
+        ),
+        out_shape=[S((2, layers, rows, cols), BF16), S((layers, deep, narrow), BF16), *(S(t.shape, F32) for t in (*m, *v))],
+        compiler_params=pltpu.CompilerParams(vmem_limit_bytes=62 * 2**20),
+        name="adam",
+    )(lax.axis_index("dp").reshape(1), *w, *sums, *m, *v)
+    return outs[0], outs[1], outs[2:]
+
+
+def gather_kernel(side, layers, *refs):
+    own_gu, own_d = refs[:2]
+    new_gu, new_d = refs[2 : 2 + layers], refs[2 + layers : 2 + 2 * layers]
+    send_gu, recv_gu, send_d, recv_d = refs[2 + 2 * layers :]
     here = Torus(side)
-    place, wrap, device, sign, me, row, col = here.place, here.wrap, here.device, here.sign, here.me, here.row, here.col
+    place, wrap, device, sign, row, col = here.place, here.wrap, here.device, here.sign, here.row, here.col
     steps = side - 1
-    rows, cols = m_gate.shape[1:]
-    deep = m_down.shape[1]
+    cols = own_gu.shape[3]
+    quarter = own_d.shape[1] // QUARTERS
     width = cols // PIECES // QUARTERS
-    at, deep_at = pl.ds(pl.multiple_of(me * rows, 8), rows), pl.ds(pl.multiple_of(me * deep, 8), deep)
-    olds = [
-        pltpu.make_async_copy(w_gate.at[:, at], old_gu.at[0], keep_sem.at[0, 0]),
-        pltpu.make_async_copy(w_up.at[:, at], old_gu.at[1], keep_sem.at[0, 1]),
-        pltpu.make_async_copy(w_down.at[:, deep_at], old_d, keep_sem.at[1, 0]),
-    ]
-    for one in olds:
-        one.start()
+    for l in range(layers):
+        new_gu[l][:, row, col] = own_gu[:, l]
+        for q in range(QUARTERS):
+            new_d[l][row, col, q] = own_d[l, q * quarter : (q + 1) * quarter]
     here.greet()
-    for one in olds:
-        one.wait()
 
     def lanes(h, q):
         return pl.ds(pl.multiple_of((h * QUARTERS + q) * width, 128), width)
@@ -395,61 +426,33 @@
             lax.fori_loop(0, PIECES, lambda h, _: (f(l, h), _)[1], 0)
             f(l, None)
 
-    total = jnp.sum(squares[...])
-    factor = jnp.minimum(1.0, 0.5 * lax.rsqrt(jnp.full((1, 128), total, F32) / count + 1e-30))
-
     def gather(l, h, q, s):
         mu, mv = place(q)
         g = sign(q)
+        gu, down = new_gu[l], new_d[l]
         if s < steps:
             v = wrap(mv - g * s)
             a, b = (mu, v) if q < 2 else (v, mu)
-            dst = new_d.at[l, a, b, q] if h is None else new_gu.at[:, l, a, b, :, lanes(h, q)]
-            src = dst
+            src = dst = down.at[a, b, q] if h is None else gu.at[:, a, b, :, lanes(h, q)]
             if s == 0:
-                src = own_d.at[l, q] if h is None else own_gu.at[:, l, :, lanes(h, q)]
+                src = own_d.at[l, pl.ds(q * quarter, quarter)] if h is None else own_gu.at[:, l, :, lanes(h, q)]
             to = device(q, mu, mv + g)
         else:
             u = wrap(mu - g * (s - steps))
             if h is None:
-                dst = new_d.at[l, u, :, q] if q < 2 else new_d.at[l, :, u, q]
+                dst = down.at[u, :, q] if q < 2 else down.at[:, u, q]
             else:
-                at = lanes(h, q)
-                dst = new_gu.at[:, l, u, :, :, at] if q < 2 else new_gu.at[:, l, :, u, :, at]
+                dst = gu.at[:, u, :, :, lanes(h, q)] if q < 2 else gu.at[:, :, u, :, lanes(h, q)]
             src = dst
             to = device(q, mu + g, mv)
         a, b = sems(l, h, q, s)
         return pltpu.make_async_remote_copy(src, dst, a, b, device_id=to, device_id_type=MESH)
 
-    def keep(l, d):
-        if d:
-            return pltpu.make_async_copy(own_d.at[l], new_d.at[l, row, col], keep_sem.at[l, 1])
-        return pltpu.make_async_copy(own_gu.at[:, l], new_gu.at[:, l, row, col], keep_sem.at[l, 0])
-
-    for l in reversed(range(layers)):
-        for h in range(PIECES):
-            for q in range(QUARTERS):
-                at = pl.ds((h * QUARTERS + q) * width, width)
-                by = jnp.tile(factor, (1, width // 128))
-                for k, (w, m, v, nm, nv) in enumerate(((old_gu.at[0], m_gate, v_gate, nm_gate, nv_gate), (old_gu.at[1], m_up, v_up, nm_up, nv_up))):
-                    new, nm[l, :, at], nv[l, :, at] = adamw(
-                        w[l, :, at].astype(F32), m[l, :, at], v[l, :, at], sum_gu[k, l, :, at] * by)
-                    own_gu[k, l, :, at] = new
-                gather(l, h, q, 0).start()
-        keep(l, False).start()
-        turned = sum_d[l].T
+    def begin(l, h):
         for q in range(QUARTERS):
-            rows = m_down.shape[1] // QUARTERS
-            at = pl.ds(q * rows, rows)
-            by = jnp.tile(factor, (1, m_down.shape[2] // 128))
-            new, nm_down[l, at], nv_down[l, at] = adamw(
-                old_d[l, at].astype(F32), m_down[l, at], v_down[l, at], turned[q * rows : (q + 1) * rows] * by)
-            own_d[l, q] = new
-            gather(l, None, q, 0).start()
-        keep(l, True).start()
-    for l in reversed(range(layers)):
-        keep(l, False).wait()
-        keep(l, True).wait()
+            gather(l, h, q, 0).start()
+
+    jobs(begin)
     for s in range(2 * steps):
         def advance(l, h, s=s):
             for q in range(QUARTERS):
@@ -460,39 +463,56 @@
         jobs(advance)
 
 
-def gather(side, sums, w, m, v):
-    layers, rows, cols = m[0].shape
-    deep, narrow = m[2].shape[1:]
-    quarter = deep // QUARTERS
+def gather(side, own_gu, own_d):
+    layers, rows, cols = own_gu.shape[1:]
+    deep, narrow = own_d.shape[1:]
     n = side * side
     steps = side - 1
-    count = layers * n * (2 * rows * cols + deep * narrow)
-    vmem, hbm = pl.BlockSpec(memory_space=pltpu.VMEM), pl.BlockSpec(memory_space=pl.ANY)
+    vmem = pl.BlockSpec(memory_space=pltpu.VMEM)
+    S = jax.ShapeDtypeStruct
     outs = pl.pallas_call(
-        functools.partial(gather_kernel, side, layers, count),
-        out_shape=[
-            jax.ShapeDtypeStruct((2, layers, side, side, rows, cols), BF16),
-            jax.ShapeDtypeStruct((layers, side, side, QUARTERS, quarter, narrow), BF16),
-            *(jax.ShapeDtypeStruct(t.shape, F32) for t in (*m, *v)),
-        ],
-        in_specs=[vmem] * 3 + [hbm] * 3 + [vmem] * 6,
-        out_specs=[hbm] * 2 + [vmem] * 6,
+        functools.partial(gather_kernel, side, layers),
+        out_shape=[S((2, side, side, rows, cols), BF16)] * layers + [S((side, side, QUARTERS, deep // QUARTERS, narrow), BF16)] * layers,
+        in_specs=[vmem] * 2,
+        out_specs=[vmem] * (2 * layers),
         scratch_shapes=[
-            pltpu.VMEM((2, layers, rows, cols), BF16),
-            pltpu.VMEM((layers, QUARTERS, quarter, narrow), BF16),
-            pltpu.VMEM((2, layers, rows, cols), BF16),
-            pltpu.VMEM((layers, deep, narrow), BF16),
             pltpu.SemaphoreType.DMA((layers, PIECES, QUARTERS, 2 * steps)),
             pltpu.SemaphoreType.DMA((layers, PIECES, QUARTERS, 2 * steps)),
             pltpu.SemaphoreType.DMA((layers, QUARTERS, 2 * steps)),
             pltpu.SemaphoreType.DMA((layers, QUARTERS, 2 * steps)),
-            pltpu.SemaphoreType.DMA((layers, 2)),
         ],
-        compiler_params=pltpu.CompilerParams(collective_id=1, has_side_effects=True, vmem_limit_bytes=40 * 2**20),
+        compiler_params=pltpu.CompilerParams(collective_id=1, has_side_effects=True, vmem_limit_bytes=4 * 2**20),
         name="gather",
-    )(*sums, *w, *m, *v)
-    gu = outs[0].reshape(2, layers, n * rows, cols)
-    return (gu[0], gu[1], outs[1].reshape(layers, n * deep, narrow), *outs[2:])
+    )(own_gu, own_d)
+    gus, downs = outs[:layers], outs[layers:]
+    return finish([t.reshape(2, n * rows, cols) for t in gus], [t.reshape(n * deep, narrow) for t in downs])
+
+
+def finish_kernel(layers, *refs):
+    gus, downs, (gate, up, down, sem) = refs[:layers], refs[layers : 2 * layers], refs[2 * layers :]
+    copies = []
+    for l in range(layers):
+        for k, (x, y) in enumerate(((gus[l].at[0], gate), (gus[l].at[1], up), (downs[l], down))):
+            copies.append(pltpu.make_async_copy(x, y.at[l], sem.at[l, k]))
+    for one in copies:
+        one.start()
+    for one in copies:
+        one.wait()
+
+
+def finish(gus, downs):
+    S = jax.ShapeDtypeStruct
+    layers = len(gus)
+    gate, down = S((layers, *gus[0].shape[1:]), BF16), S((layers, *downs[0].shape), BF16)
+    return pl.pallas_call(
+        functools.partial(finish_kernel, layers),
+        out_shape=[gate, gate, down],
+        in_specs=[pl.BlockSpec(memory_space=pltpu.VMEM)] * (2 * layers),
+        out_specs=[pl.BlockSpec(memory_space=pl.ANY)] * 3,
+        scratch_shapes=[pltpu.SemaphoreType.DMA((layers, 3))],
+        compiler_params=pltpu.CompilerParams(vmem_limit_bytes=2**20),
+        name="finish",
+    )(*gus, *downs)
 
 
 def solution(mesh):
@@ -505,7 +525,8 @@
         a0, a0t, h1, a1, a1t, dyt = forward(x[0], dy[0], *weights)
         acts = (h1, a1, a1t, dy[0], dyt, a0, a0t)
         sums = backward(side, weights[0].shape[0], acts, weights, m[0].shape[1], m[2].shape[1])
-        return gather(side, sums, weights, m, v)
+        own_gu, own_d, moments = adam(sums, weights, m, v, side * side)
+        return (*gather(side, own_gu, own_d), *moments)
 
     whole, block = P(None, None, None), P(None, "dp", None)
     return jax.shard_map(

time: 311 us -> 290 us (0.932)
  local copies, waits for them, and re-layouts: 31.1 us -> 2.05 us
  Pallas kernels: 278 us -> 287 us
    unnamed x29 -> x4, local copies, waits for them, and re-layouts: 20.8 us -> 2.05 us
    pallas_call x1 -> x3, Pallas kernels: 78.3 us -> 91.4 us  [the longest x1 80 us: gather(): pl.pallas_call(functools.partial(gather_kernel, side, layers), out_shape=...]
    slice x1 -> x0, local copies, waits for them, and re-layouts: 10.3 us -> none  [gather(): return (gu[0], gu[1], outs[1].reshape(layers, n * deep, narrow), *outs[2:])]
    pallas_call x1, Pallas kernels: 172 us -> 168 us  [backward(): pl.pallas_call(functools.partial(backward_kernel, side, layers), out_shap...]
where the time goes in v2:
time: 290 us
  Pallas kernels  287 us (99%)
    pallas_call x1, Pallas kernels, backward(): pl.pallas_call(functools.partial(backward_kernel, side, layers), out_shap...  168 us
    pallas_call x1, Pallas kernels, gather(): pl.pallas_call(functools.partial(gather_kernel, side, layers), out_shape=...  80 us
    pallas_call x1, Pallas kernels, forward(): pl.pallas_call(forward_kernel, grid=(n // T,), in_specs=[tile, tile, cons...  27.9 us

profile of v2, /device:TPU:96, one launch (start us, length us, event | category | flops | bytes accessed | tf_op | source)
XLA Modules:
  0.0 290.2 jit_solution(5354221796330003800)
XLA Ops:
  0.6 27.9 %fwd.1 = (bf16[2048,640]{1,0:T(8,128)(2,1)}, bf16[640,2048]{1,0:T(8,128)(2,1)}, bf16[2048,640]{1,0:T(8,128)(2,1)}, bf16[2048,640]{1,0:T(8,128)(2,1)}, bf16[640,2...) custom-call(bf16[2048,640]{1,0:T(8,128)(2,1)} %bitcast.13, bf16[2048,640]{1,0:T(8,128)(2,1)} %bitcast.11, ...), custom_call_target="tpu_custom_call" | custom-call | tf_op jit(solution)/shard_map/fwd/pallas_call | solution.py:51
  28.5 168.0 %bwd.1 = (f32[2,2,40,2048]{3,2,1,0:T(8,128)}, f32[2,640,128]{2,1,0:T(8,128)}, f32[8,128]{1,0:T(8,128)}) custom-call(bf16[2048,640]{1,0:T(8,128)(2,1)} %get-tuple-element.33.refs_0_, bf16[2048,640]{1,0:T(8,128)(2,1)} %get-tuple-element.34.refs_1_, bf16[640,2048]{1,0:T(8,128)(2,1)} %get-tuple-element.35.refs_2_, bf16[2048,640]{1,0:T(8,128)(2,1)} %bitcast.12, ...), custom_call_target="tpu_custom_call" | custom-call | tf_op jit(solution)/shard_map/bwd/pallas_call | solution.py:337
  196.5 5.7 %adam.1 = (bf16[2,2,40,2048]{3,2,1,0:T(8,128)(2,1)}, bf16[2,128,640]{2,1,0:T(8,128)(2,1)}, f32[2,40,2048]{2,1,0:T(8,128)}, f32[2,40,2048]{2,1,0:T(8,128)}, f32[2...) custom-call(s32[1]{0:T(128)} %bitcast.me, ...), custom_call_target="tpu_custom_call" | custom-call | tf_op jit(solution)/shard_map/adam/pallas_call | solution.py:385
  202.3 0.0 copy-start
  202.3 1.1 copy-done
  203.3 0.0 copy-start.1
  203.4 1.0 copy-done.1
  204.3 80.0 %gather.1 = (bf16[2,4,4,40,2048]{4,3,2,1,0:T(8,128)(2,1)S(1)}, bf16[2,4,4,40,2048]{4,3,2,1,0:T(8,128)(2,1)S(1)}, bf16[4,4,4,32,640]{4,3,2,1,0:T(8,128)(2,1)S(1)}, bf16[4,4,4,32,640]{4,3,2,1,0:T(8,128)(2,1)S(1)}) custom-call(bf16[2,2,40,2048]{3,2,1,0:T(8,128)(2,1)S(1)} %copy-done, bf16[2,128,640]{2,1,0:T(8,128)(2,1)S(1)} %copy-done.1), custom_call_target="tpu_custom_call" | custom-call | tf_op jit(solution)/shard_map/gather/pallas_call | solution.py:473
  284.3 5.6 %finish.1 = (bf16[2,640,2048]{2,1,0:T(8,128)(2,1)}, bf16[2,640,2048]{2,1,0:T(8,128)(2,1)}, bf16[2,2048,640]{2,1,0:T(8,128)(2,1)}) custom-call(bf16[2,640,2048]{2,1,0:T(8,128)(2,1)S(1)} %bitcast.7, bf16[2,640,2048]{2,1,0:T(8,128)(2,1)S(1)} %bitcast.8, bf16[2048,640]{1,0:T(8,128)(2,1)S(1)} %bitcast.9, bf16[2048,640]{1,0:T(8,128)(2,1)S(1)} %bitcast.10), custom_call_target="tpu_custom_call" | custom-call | tf_op jit(solution)/shard_map/finish/pallas_call | solution.py:507
Async XLA Ops:
  202.3 1.1 copy-start
  203.3 1.0 copy-start.1

commit v3 on v2

--- a/solution.py
+++ b/solution.py
@@ -14,7 +14,7 @@
 PIECES = 2
 CHUNKS = 4
 TILE = 512
-STEPS_AT = (((3, 3), (2, 1)), ((3, 4), (1, 0)), ((3, 5), (2, 2)))
+STEPS_AT = (((2, 1),), ((3, 3), (1, 0)), ((2, 2),))
 
 
 NT = (((1,), (1,)), ((), ()))
@@ -117,7 +117,7 @@
 def backward_kernel(side, layers, *refs):
     h1, a1, a1t, dy, dyt, a0, a0t, wg, wu, wd, sum_gu, sum_d, squares = refs[:13]
     (A, AT, DY, DYT, wgb, wub, wdb, ps, gs, us, das, loc_gu, loc_d, in1_gu, in1_d, in2_gu, in2_d, norms, tile) = refs[13:32]
-    act_sem, w_sem, send_gu, recv_gu, send_d, recv_d, norm_send, norm_recv = refs[32:]
+    act_sem, w_sem, send_gu, recv_gu, send_d, recv_d, send_p, recv_p, norm_send, norm_recv = refs[32:]
     here = Torus(side)
     place, wrap, device, sign = here.place, here.wrap, here.device, here.sign
     n, d = A.shape
@@ -127,14 +127,25 @@
     steps = side - 1
     last = layers - 1
 
+    wide = loc_d.shape[4]
+
+    def across(k, i):
+        return lax.rem(lax.rem(k, CHUNKS) + side - i, side)
+
+    def units(k, i):
+        return pl.ds(pl.multiple_of((i * side + across(k, i)) * wide, 128), wide)
+
     def weights(k):
-        l, c, slot = last - lax.div(k, CHUNKS), lax.rem(k, CHUNKS), lax.rem(k, 2)
-        cs = pl.ds(pl.multiple_of(c * F, F), F)
-        return [
-            pltpu.make_async_copy(wg.at[l, :, cs], wgb.at[slot], w_sem.at[slot, 0]),
-            pltpu.make_async_copy(wu.at[l, :, cs], wub.at[slot], w_sem.at[slot, 1]),
-            pltpu.make_async_copy(wd.at[l, cs], wdb.at[slot], w_sem.at[slot, 2]),
-        ]
+        l, slot = last - lax.div(k, CHUNKS), lax.rem(k, 2)
+        copies = []
+        for i in range(side):
+            of, to = units(k, i), pl.ds(i * wide, wide)
+            copies += [
+                pltpu.make_async_copy(wg.at[l, :, of], wgb.at[slot, :, to], w_sem.at[slot, 0, i]),
+                pltpu.make_async_copy(wu.at[l, :, of], wub.at[slot, :, to], w_sem.at[slot, 1, i]),
+                pltpu.make_async_copy(wd.at[l, of], wdb.at[slot, to], w_sem.at[slot, 2, i]),
+            ]
+        return copies
 
     loads = [pltpu.make_async_copy(x, y, act_sem.at[k]) for k, (x, y) in enumerate(((a1, A), (dy, DY), (a1t, AT), (dyt, DYT)))]
     for one in (loads[0], loads[1], *weights(0), loads[2], loads[3]):
@@ -149,63 +160,80 @@
         return pl.ds(q * (d // QUARTERS), d // QUARTERS)
 
     def lanes(k, q):
-        return pl.ds(pl.multiple_of((lax.rem(k, CHUNKS) * QUARTERS + q) * width, 128), width)
+        return units(k, q)
 
     def sems(gu, k, q, s):
         return (send_gu.at[k, q, s], recv_gu.at[k, q, s]) if gu else (send_d.at[k, q, s], recv_d.at[k, q, s])
 
-    def local_unit(gu, k, q, u):
-        if not gu:
-            return loc_d.at[k, u, :, strip(q)] if q < 2 else loc_d.at[k, :, u, strip(q)]
-        return loc_gu.at[:, u, :, :, lanes(k, q)] if q < 2 else loc_gu.at[:, :, u, :, lanes(k, q)]
-
-    def first(gu, k, q, s):
+    def first(k, q, s):
         mu, mv = place(q)
         g = sign(q)
-        ins = in1_gu if gu else in1_d
-        src = local_unit(gu, k, q, wrap(mu - g)) if s == 0 else ins.at[k, q, s - 1]
-        a, b = sems(gu, k, q, s)
-        return pltpu.make_async_remote_copy(src, ins.at[k, q, s], a, b, device_id=device(q, mu + g, mv), device_id_type=MESH)
+        if s == 0:
+            u = wrap(mu - g)
+            src = loc_gu.at[:, u, :, :, lanes(k, q)] if q < 2 else loc_gu.at[:, :, u, :, lanes(k, q)]
+        else:
+            src = in1_gu.at[k, q, s - 1]
+        a, b = sems(True, k, q, s)
+        return pltpu.make_async_remote_copy(src, in1_gu.at[k, q, s], a, b, device_id=device(q, mu + g, mv), device_id_type=MESH)
+
+    def piece(k, q, s):
+        l = last - lax.div(k, CHUNKS)
+        mu, mv = place(q)
+        g = sign(q)
+        u = wrap(mu - g * (s + 1))
+        v = across(k, u)
+        if s == 0:
+            src = loc_d.at[l, u, v, strip(q)] if q < 2 else loc_d.at[l, v, u, strip(q)]
+        else:
+            src = in1_d.at[l, q, s - 1, v]
+        return pltpu.make_async_remote_copy(
+            src, in1_d.at[l, q, s, v], send_p.at[k, q, s], recv_p.at[k, q, s], device_id=device(q, mu + g, mv), device_id_type=MESH)
 
     def second(gu, k, q, s):
         mu, mv = place(q)
-        g = sign(q)
-        ins = in2_gu if gu else in2_d
-        if s == 0:
-            v = wrap(mv - g)
-            src = in1_gu.at[k, q, steps - 1, :, v] if gu else in1_d.at[k, q, steps - 1, v]
-        else:
-            src = ins.at[k, q, s - 1]
-        a, b = sems(gu, k, q, steps + s)
-        return pltpu.make_async_remote_copy(src, ins.at[k, q, s], a, b, device_id=device(q, mu, mv + g), device_id_type=MESH)
-
-    def add_first(gu, k, q, s):
+        v = wrap(mv + sign(q) * (s + 1))
+        src, dst = (in1_gu.at[k, q, steps - 1, :, v], in2_gu.at[k, q, s]) if gu else (in1_d.at[k, q, steps - 1, v], in2_d.at[k, q, s])
+        a, b = sems(gu, k, q, steps + s if gu else s)
+        return pltpu.make_async_remote_copy(src, dst, a, b, device_id=device(q, mu, v), device_id_type=MESH)
+
+    def add_first(k, q, s):
         u = wrap(place(q)[0] - sign(q) * (s + 2))
 
         def one(v, _):
             a, b = (u, v) if q < 2 else (v, u)
-            if gu:
-                mine = loc_gu[:, a, b, :, lanes(k, q)].astype(F32)
-                in1_gu[k, q, s, :, v] = (in1_gu[k, q, s, :, v].astype(F32) + mine).astype(BF16)
-            else:
-                mine = loc_d[k, a, b, strip(q)].astype(F32)
-                in1_d[k, q, s, v] = (in1_d[k, q, s, v].astype(F32) + mine).astype(BF16)
+            mine = loc_gu[:, a, b, :, lanes(k, q)].astype(F32)
+            in1_gu[k, q, s, :, v] = (in1_gu[k, q, s, :, v].astype(F32) + mine).astype(BF16)
             return _
 
-        lax.fori_loop(0, side, one, 0)
-
-    def add_second(gu, k, q, s):
-        v = wrap(place(q)[1] - sign(q) * (s + 2))
+        if s < steps - 1:
+            lax.fori_loop(0, side, one, 0)
+        else:
+            lax.fori_loop(1, side, lambda v, _: one(wrap(place(q)[1] + v), _), 0)
+
+    def add_piece(k, q, s):
+        l = last - lax.div(k, CHUNKS)
+        u = wrap(place(q)[0] - sign(q) * (s + 2))
+        v = across(k, u)
+        a, b = (u, v) if q < 2 else (v, u)
+
+        def add():
+            mine = loc_d[l, a, b, strip(q)].astype(F32)
+            in1_d[l, q, s, v] = (in1_d[l, q, s, v].astype(F32) + mine).astype(BF16)
+
+        if s < steps - 1:
+            add()
+        else:
+            pl.when(v != place(q)[1])(add)
+
+    def add_second(gu, k, q):
+        mv = place(q)[1]
         if gu:
-            total = (in2_gu[k, q, s].astype(F32) + in1_gu[k, q, steps - 1, :, v].astype(F32)).astype(BF16)
-        else:
-            total = (in2_d[k, q, s].astype(F32) + in1_d[k, q, steps - 1, v].astype(F32)).astype(BF16)
-        if s < steps - 1:
-            if gu:
-                in2_gu[k, q, s] = total
-            else:
-                in2_d[k, q, s] = total
-            return
+            total = loc_gu[:, here.row, here.col, :, lanes(k, q)].astype(F32) + in1_gu[k, q, steps - 1, :, mv].astype(F32)
+        else:
+            total = loc_d[k, here.row, here.col, strip(q)].astype(F32) + in1_d[k, q, steps - 1, mv].astype(F32)
+        for s in range(steps):
+            total += (in2_gu if gu else in2_d)[k, q, s].astype(F32)
+        total = total.astype(BF16)
         total = total.astype(F32)
         if gu:
             sum_gu[:, last - lax.div(k, CHUNKS), :, lanes(k, q)] = total
@@ -215,24 +243,37 @@
         square = square.reshape(-1, 8, square.shape[-1]).sum(0)
         tile[...] += sum(square[:, i : i + 128] for i in range(0, square.shape[-1], 128))
 
-    def begin(gu, k):
+    def begin(k):
         for q in range(QUARTERS):
-            first(gu, k, q, 0).start()
+            first(k, q, 0).start()
+            piece(k, q, 0).start()
+
+    def turn_down(l):
+        for q in range(QUARTERS):
+            for s in range(steps):
+                second(False, l, q, s).start()
 
     def advance(gu, k, s):
         for q in range(QUARTERS):
             if s < steps:
-                first(gu, k, q, s).wait()
-                add_first(gu, k, q, s)
-                (first(gu, k, q, s + 1) if s + 1 < steps else second(gu, k, q, 0)).start()
+                first(k, q, s).wait()
+                add_first(k, q, s)
+                if s + 1 < steps:
+                    first(k, q, s + 1).start()
+                else:
+                    for i in range(steps):
+                        second(True, k, q, i).start()
+                piece(k, q, s).wait()
+                add_piece(k, q, s)
+                if s + 1 < steps:
+                    piece(k, q, s + 1).start()
             else:
-                second(gu, k, q, s - steps).wait()
-                add_second(gu, k, q, s - steps)
-                if s + 1 < 2 * steps:
-                    second(gu, k, q, s - steps + 1).start()
+                for i in range(steps):
+                    second(gu, k, q, i).wait()
+                add_second(gu, k, q)
 
     def chunk(k, inner):
-        slot, c = lax.rem(k, 2), lax.rem(k, CHUNKS)
+        slot = lax.rem(k, 2)
         for one in weights(k):
             one.wait()
 
@@ -264,23 +305,20 @@
                 for one in loads[2:]:
                     one.wait()
 
-        cs = pl.ds(pl.multiple_of(c * F, F), F)
         rows = loc_gu.shape[3]
         for which, of in ((0, gs), (1, us)):
             g = dot(AT[...], of[...]).astype(BF16)
             for i in range(side * side):
-                loc_gu[which, i // side, i % side, :, cs] = g[i * rows : (i + 1) * rows]
+                for j in range(side):
+                    loc_gu[which, i // side, i % side, :, units(k, j)] = g[i * rows : (i + 1) * rows, j * wide : (j + 1) * wide]
         l = last - lax.div(k, CHUNKS)
         g = dot(DYT[...], ps[...]).astype(BF16)
-        wide = loc_d.shape[4]
-        for i in range(F // wide):
-            to = c * (F // wide) + i
-            loc_d[l, lax.div(to, side), lax.rem(to, side)] = g[:, i * wide : (i + 1) * wide]
+        for i in range(side):
+            loc_d[l, i, across(k, i)] = g[:, i * wide : (i + 1) * wide]
         ticks(2)
-        begin(True, k)
+        begin(k)
 
     lax.fori_loop(0, CHUNKS, lambda k, _: (chunk(k, True), _)[1], 0)
-    begin(False, last)
 
     again = [pltpu.make_async_copy(x, y, act_sem.at[k]) for k, (x, y) in enumerate(((h1, A), (a0, A), (a0t, AT)))]
     again[0].start()
@@ -301,17 +339,20 @@
 
     def outer(k, _):
         chunk(k, False)
-        for i in range(CHUNKS):
-            pl.when(k == CHUNKS + i)(lambda: advance(False, last, i))
+
+        pl.when(k == CHUNKS + 1)(lambda: turn_down(last))
+        pl.when(k == CHUNKS + 2)(lambda: advance(False, last, steps))
         return _
 
-    lax.fori_loop(CHUNKS, 2 * CHUNKS, outer, 0)
-    begin(False, 0)
-    end = 2 * CHUNKS - 1
-    for s in range(2 * steps):
-        for gu, k, done in ((True, end - 2, 3), (False, last, CHUNKS), (True, end - 1, 1), (True, end, 0), (False, 0, 0)):
-            if done + s < 2 * steps:
-                advance(gu, k, done + s)
+    lax.fori_loop(CHUNKS, layers * CHUNKS, outer, 0)
+    end = layers * CHUNKS - 1
+    for s in range(steps + 1):
+        for k, done in ((end - 2, 3), (end - 1, 1), (end, 0)):
+            if done + s <= steps:
+                advance(True, k, done + s)
+        if s == steps - 1:
+            turn_down(0)
+    advance(False, 0, steps)
 
     norms[here.me] = tile[...]
 
@@ -330,6 +371,7 @@
     f = weights[0].shape[2]
     F = f // CHUNKS
     width = F // QUARTERS
+    assert CHUNKS == QUARTERS == side and width == deep
     steps = side - 1
     S, V = jax.ShapeDtypeStruct, pltpu.VMEM
     jobs = layers * CHUNKS
@@ -351,11 +393,13 @@
             V((layers, QUARTERS, steps, d // QUARTERS, deep), BF16),
             V((side * side, 8, 128), F32), V((8, 128), F32),
             pltpu.SemaphoreType.DMA((4,)),
-            pltpu.SemaphoreType.DMA((2, 3)),
+            pltpu.SemaphoreType.DMA((2, 3, side)),
             pltpu.SemaphoreType.DMA((jobs, QUARTERS, 2 * steps)),
             pltpu.SemaphoreType.DMA((jobs, QUARTERS, 2 * steps)),
-            pltpu.SemaphoreType.DMA((layers, QUARTERS, 2 * steps)),
-            pltpu.SemaphoreType.DMA((layers, QUARTERS, 2 * steps)),
+            pltpu.SemaphoreType.DMA((layers, QUARTERS, steps)),
+            pltpu.SemaphoreType.DMA((layers, QUARTERS, steps)),
+            pltpu.SemaphoreType.DMA((jobs, QUARTERS, steps)),
+            pltpu.SemaphoreType.DMA((jobs, QUARTERS, steps)),
             pltpu.SemaphoreType.DMA((side * side,)),
             pltpu.SemaphoreType.DMA((side * side,)),
         ],

time: 290 us -> 286 us (0.986)
  Pallas kernels: 287 us -> 283 us
    pallas_call x1, Pallas kernels: 168 us -> 162 us  [backward(): pl.pallas_call(functools.partial(backward_kernel, side, layers), out_shap...]
where the time goes in v3:
time: 286 us
  Pallas kernels  283 us (99%)
    pallas_call x1, Pallas kernels, backward(): pl.pallas_call(functools.partial(backward_kernel, side, layers), out_shap...  162 us
    pallas_call x1, Pallas kernels, gather(): pl.pallas_call(functools.partial(gather_kernel, side, layers), out_shape=...  82.4 us
    pallas_call x1, Pallas kernels, forward(): pl.pallas_call(forward_kernel, grid=(n // T,), in_specs=[tile, tile, cons...  27.9 us

profile of v3, /device:TPU:96, one launch (start us, length us, event | category | flops | bytes accessed | tf_op | source)
XLA Modules:
  0.0 286.2 jit_solution(7333368448841154610)
XLA Ops:
  0.6 27.9 %fwd.1 = (bf16[2048,640]{1,0:T(8,128)(2,1)}, bf16[640,2048]{1,0:T(8,128)(2,1)}, bf16[2048,640]{1,0:T(8,128)(2,1)}, bf16[2048,640]{1,0:T(8,128)(2,1)}, bf16[640,2...) custom-call(bf16[2048,640]{1,0:T(8,128)(2,1)} %bitcast.13, bf16[2048,640]{1,0:T(8,128)(2,1)} %bitcast.11, ...), custom_call_target="tpu_custom_call" | custom-call | tf_op jit(solution)/shard_map/fwd/pallas_call | solution.py:51
  28.5 161.9 %bwd.1 = (f32[2,2,40,2048]{3,2,1,0:T(8,128)}, f32[2,640,128]{2,1,0:T(8,128)}, f32[8,128]{1,0:T(8,128)}) custom-call(bf16[2048,640]{1,0:T(8,128)(2,1)} %get-tuple-element.33.refs_0_, bf16[2048,640]{1,0:T(8,128)(2,1)} %get-tuple-element.34.refs_1_, bf16[640,2048]{1,0:T(8,128)(2,1)} %get-tuple-element.35.refs_2_, bf16[2048,640]{1,0:T(8,128)(2,1)} %bitcast.12, ...), custom_call_target="tpu_custom_call" | custom-call | tf_op jit(solution)/shard_map/bwd/pallas_call | solution.py:379
  190.4 5.5 %adam.1 = (bf16[2,2,40,2048]{3,2,1,0:T(8,128)(2,1)}, bf16[2,128,640]{2,1,0:T(8,128)(2,1)}, f32[2,40,2048]{2,1,0:T(8,128)}, f32[2,40,2048]{2,1,0:T(8,128)}, f32[2...) custom-call(s32[1]{0:T(128)} %bitcast.me, ...), custom_call_target="tpu_custom_call" | custom-call | tf_op jit(solution)/shard_map/adam/pallas_call | solution.py:429
  195.9 0.0 copy-start
  195.9 1.1 copy-done
  197.0 0.0 copy-start.1
  197.0 1.0 copy-done.1
  197.9 82.4 %gather.1 = (bf16[2,4,4,40,2048]{4,3,2,1,0:T(8,128)(2,1)S(1)}, bf16[2,4,4,40,2048]{4,3,2,1,0:T(8,128)(2,1)S(1)}, bf16[4,4,4,32,640]{4,3,2,1,0:T(8,128)(2,1)S(1)}, bf16[4,4,4,32,640]{4,3,2,1,0:T(8,128)(2,1)S(1)}) custom-call(bf16[2,2,40,2048]{3,2,1,0:T(8,128)(2,1)S(1)} %copy-done, bf16[2,128,640]{2,1,0:T(8,128)(2,1)S(1)} %copy-done.1), custom_call_target="tpu_custom_call" | custom-call | tf_op jit(solution)/shard_map/gather/pallas_call | solution.py:517
  280.4 5.6 %finish.1 = (bf16[2,640,2048]{2,1,0:T(8,128)(2,1)}, bf16[2,640,2048]{2,1,0:T(8,128)(2,1)}, bf16[2,2048,640]{2,1,0:T(8,128)(2,1)}) custom-call(bf16[2,640,2048]{2,1,0:T(8,128)(2,1)S(1)} %bitcast.7, bf16[2,640,2048]{2,1,0:T(8,128)(2,1)S(1)} %bitcast.8, bf16[2048,640]{1,0:T(8,128)(2,1)S(1)} %bitcast.9, bf16[2048,640]{1,0:T(8,128)(2,1)S(1)} %bitcast.10), custom_call_target="tpu_custom_call" | custom-call | tf_op jit(solution)/shard_map/finish/pallas_call | solution.py:551
Async XLA Ops:
  195.9 1.1 copy-start
  197.0 1.0 copy-start.1
